TPU v7x, 256 devices: a whole 4x4x8 slice. The times are simulated.
256 devices in a mesh: row: 8 (over y, core), col: 32 (over x, z).
Axes of the slice: x: 4, y: 4, z: 8, core: 2. Of those that a mesh axis runs over, the one named last changes fastest.
Arguments:
- inner_base: bfloat16 [4, 1, 2, 4096, 14336], P(None, None, None, 'row', 'col'), may hold values from -250 to 250
- inner_left: bfloat16 [4, 1, 2, 4096, 16], P(None, None, None, ('row', 'col')), may hold values from -6 to 6
- inner_right: bfloat16 [4, 1, 2, 16, 14336], P(None, None, None, 'row', 'col'), may hold values from -12 to 12
- inner_mag: float32 [4, 1, 2, 14336], P(None, None, None, 'col'), may hold values from 512 to 2048
- outer_base: bfloat16 [4, 1, 14336, 4096], P(None, None, 'row', 'col'), may hold values from -250 to 250
- outer_left: bfloat16 [4, 1, 14336, 16], P(None, None, ('row', 'col')), may hold values from -6 to 6
- outer_right: bfloat16 [4, 1, 16, 4096], P(None, None, 'row', 'col'), may hold values from -12 to 12
- outer_mag: float32 [4, 1, 4096], P(None, None, 'col'), may hold values from 1792 to 7168
Outputs:
- inner_merged: bfloat16 [4, 1, 2, 4096, 14336], P(None, None, None, 'row', 'col')
- outer_merged: bfloat16 [4, 1, 14336, 4096], P(None, None, 'row', 'col')
All inputs are finite; a program needn't handle non-finite values.
Results may differ from a plain program's by a relative error of at most 0.001.
Values may be sent and summed in bfloat16 or wider, within the bound.
No kernel may reach another device: no remote copies, remote signals or barrier semaphores. Data moves between devices by JAX's collectives and lax.ppermute only.
A program may use at most 64 MiB of HBM per device.

v0:
```python
import jax
import jax.numpy as jnp
from jax import lax
from jax.sharding import PartitionSpec as P

epsilon = 1e-06


def from_everyone(value, axis):
    size = lax.axis_size(axis)
    return lax.all_to_all(
        jnp.broadcast_to(value[None], (size, *value.shape)), axis, 0, 0, tiled=True
    )


def over_copies(value, axis):
    return from_everyone(value, axis).sum(axis=0)


def packed_total(arrays, axis):
    line, at, finished = (jnp.concatenate([a.reshape(-1) for a in arrays]), 0, [])
    subtotal = over_copies(line, axis)
    for a in arrays:
        finished.append(subtotal[at : at + a.size].reshape(a.shape))
        at += a.size
    return tuple(finished)


def in_order(tiles, dim):
    lengths = list(tiles.shape[1:])
    lengths[dim] *= tiles.shape[0]
    return jnp.moveaxis(tiles, 0, dim).reshape(lengths)


def gathered_copies(value, axis, dim):
    tiles = from_everyone(value, axis)
    return in_order(tiles, dim)


def turned_gather(arrays, axis, dims):
    turned = [jnp.moveaxis(a, dim, 0) for a, dim in zip(arrays, dims)]
    both = jnp.concatenate([t.reshape(len(t), -1) for t in turned], axis=1)
    result, at, finished = (lax.all_gather(both, axis, axis=0, tiled=True), 0, [])
    for t, dim in zip(turned, dims):
        section = result[:, at : at + t[0].size].reshape(-1, *t.shape[1:])
        finished.append(jnp.moveaxis(section, 0, dim))
        at += t[0].size
    return tuple(finished)


def combine_tile(base, left, right):
    delta = jnp.einsum("...ik,...kj->...ij", left, right, preferred_element_type=jnp.float32)
    return base.astype(jnp.float32) + delta


def merge_layer(
    inner_base, outer_base, inner_mag, outer_mag, inner_left, outer_left, inner_right, outer_right
):
    inner_full = combine_tile(inner_base, inner_left, inner_right)
    outer_full = combine_tile(outer_base, outer_left, outer_right)
    inner_squares = jnp.sum(inner_full * inner_full, axis=-2)
    outer_squares = jnp.sum(outer_full * outer_full, axis=-2)
    inner_totals, outer_totals = packed_total((inner_squares, outer_squares), "row")
    inner_scale = lax.rsqrt(inner_totals + epsilon)
    outer_scale = lax.rsqrt(outer_totals + epsilon)
    inner_factor = inner_mag * inner_scale
    outer_factor = outer_mag * outer_scale
    inner_merged = (inner_factor[..., None, :] * inner_full).astype(jnp.bfloat16)
    outer_merged = (outer_factor[..., None, :] * outer_full).astype(jnp.bfloat16)
    return (inner_merged, outer_merged)


def shards(
    inner_base, inner_left, inner_right, inner_mag, outer_base, outer_left, outer_right, outer_mag
):
    layer_count = inner_base.shape[0]
    inner_outputs = []
    outer_outputs = []
    inner_rows, outer_rows = (
        gathered_copies(inner_left, "col", 3),
        gathered_copies(outer_left, "col", 2),
    )
    inner_ranks, outer_ranks = turned_gather((inner_right, outer_right), "row", (3, 2))
    for layer_index in range(layer_count):
        inner_merged, outer_merged = merge_layer(
            inner_base[layer_index],
            outer_base[layer_index],
            inner_mag[layer_index],
            outer_mag[layer_index],
            inner_rows[layer_index],
            outer_rows[layer_index],
            inner_ranks[layer_index],
            outer_ranks[layer_index],
        )
        inner_outputs.append(inner_merged)
        outer_outputs.append(outer_merged)
    return (jnp.stack(inner_outputs), jnp.stack(outer_outputs))


def solution(mesh):
    in_specs = (
        P(None, None, None, "row", "col"),
        P(None, None, None, ("row", "col"), None),
        P(None, None, None, "row", "col"),
        P(None, None, None, "col"),
        P(None, None, "row", "col"),
        P(None, None, ("row", "col"), None),
        P(None, None, "row", "col"),
        P(None, None, "col"),
    )
    out_specs = (P(None, None, None, "row", "col"), P(None, None, "row", "col"))
    return jax.shard_map(shards, mesh=mesh, in_specs=in_specs, out_specs=out_specs, check_vma=False)
```

profile of v0, /device:TPU:1, one launch (start us, length us, event | category | flops | bytes accessed | tf_op | source)
XLA Modules:
  0.0 110.4 jit_solution(7065436759786785537)
XLA Ops:
  1.7 1.8 %reshape.406 = bf16[32,2,1024]{2,1,0:T(2,128)(2,1)} reshape(bf16[32,4,1,2,16,16]{5,4,3,2,1,0:T(8,128)(2,1)S(1)} %broadcast_bitcast_fusion) | data formatting | bytes 262144
  3.5 11.9 %all-to-all-start = ((bf16[32,2,1024]{2,1,0:T(2,128)(2,1)}), bf16[32,2,1024]{2,1,0:T(2,128)(2,1)S(1)}, u32[]{:S(2)}, u32[]{:S(2)}) async-start(bf16[32,2,1024]{2,1,0:T(2,128)(2,1)} %reshape.406), calls=%async_computation | async-start | bytes 262144 | tf_op jit(solution)/shard_map/all_to_all | solution.py:11
  15.7 1.6 %fusion.20 = (bf16[1,1,1792,128]{3,2,1,0:T(8,128)(2,1)S(1)}, bf16[1,1,1792,128]{3,2,1,0:T(8,128)(2,1)S(1)}, bf16[1,1,1792,128]{3,2,1,0:T(8,128)(2,1)S(1)}, bf16[1,1,1792,128]{3,2,1,0:T(8,128)(2,1)S(1)}) fusion(bf16[4,1,1792,128]{3,2,1,0:T(8,128)(2,1)} %param.12), kind=kLoop, calls=%fused_computation.68 | loop fusion | bytes 3670016 | tf_op jit(solution)/shard_map/slice | solution.py:87
  17.3 14.1 %all-gather = bf16[8,2,4096]{2,1,0:T(2,128)(2,1)S(1)} all-gather(bf16[1,2,4096]{2,1,0:T(2,128)(2,1)S(1)} %maximum_bitcast_fusion), channel_id=1, replica_groups=mesh['row'=8,'col'=32] {'row'}, dimensions={0}, use_global_device_ids=true | all-gather | bytes 147456 | tf_op jit(solution)/shard_map/all_gather | solution.py:43
  31.7 1.7 %reshape.408 = bf16[32,2,1792]{2,1,0:T(2,128)(2,1)} reshape(bf16[32,4,1,16,56]{4,3,2,1,0:T(8,128)(2,1)S(1)} %broadcast_bitcast_fusion.1) | data formatting | bytes 458752
  36.6 9.5 %all-to-all-start.1 = ((bf16[32,2,1792]{2,1,0:T(2,128)(2,1)}), bf16[32,2,1792]{2,1,0:T(2,128)(2,1)S(1)}, u32[]{:S(2)}, u32[]{:S(2)}) async-start(bf16[32,2,1792]{2,1,0:T(2,128)(2,1)} %reshape.408), calls=%async_computation.1 | async-start | bytes 458752 | tf_op jit(solution)/shard_map/all_to_all | solution.py:11
  48.8 2.9 %multiply_reduce_fusion.2 = (f32[2,448]{1,0:T(2,128)S(1)}, f32[2,512,448]{1,2,0:T(8,128)}) fusion(bf16[2,512,16]{1,2,0:T(8,128)(2,1)S(1)} %reshape.382, bf16[4,1,2,16,448]{4,3,2,1,0:T(8,128)(2,1)S(1)} %bitcast.187, bf16[4,1,2,512,448]{3,4,2,1,0:T(8,128)(2,1)} %param.8), kind=kOutput, calls=%fused_computation.19 | convolution fusion | flops 16514176 | bytes 2821632 | tf_op jit(solution)/shard_map/...ik,...kj->...ij/dot_general | solution.py:52
  51.8 2.9 %multiply_reduce_fusion.1 = (f32[2,448]{1,0:T(2,128)S(1)}, f32[2,512,448]{1,2,0:T(8,128)}) fusion(bf16[2,512,16]{1,2,0:T(8,128)(2,1)S(1)} %reshape.387, bf16[4,1,2,16,448]{4,3,2,1,0:T(8,128)(2,1)S(1)} %bitcast.188, bf16[4,1,2,512,448]{3,4,2,1,0:T(8,128)(2,1)} %param.8), kind=kOutput, calls=%fused_computation.17 | convolution fusion | flops 16514176 | bytes 2821632 | tf_op jit(solution)/shard_map/...ik,...kj->...ij/dot_general | solution.py:52
  54.8 2.9 %multiply_reduce_fusion = (f32[2,448]{1,0:T(2,128)S(1)}, f32[2,512,448]{1,2,0:T(8,128)}) fusion(bf16[2,512,16]{1,2,0:T(8,128)(2,1)S(1)} %reshape.392, bf16[4,1,2,16,448]{4,3,2,1,0:T(8,128)(2,1)S(1)} %bitcast.189, bf16[4,1,2,512,448]{3,4,2,1,0:T(8,128)(2,1)} %param.8), kind=kOutput, calls=%fused_computation.15 | convolution fusion | flops 16514176 | bytes 2821632 | tf_op jit(solution)/shard_map/...ik,...kj->...ij/dot_general | solution.py:52
  57.7 2.9 %multiply_reduce_fusion.3 = (f32[2,448]{1,0:T(2,128)S(1)}, f32[2,512,448]{1,2,0:T(8,128)}) fusion(bf16[2,512,16]{1,2,0:T(8,128)(2,1)S(1)} %reshape.376, bf16[4,1,2,16,448]{4,3,2,1,0:T(8,128)(2,1)S(1)} %bitcast.190, bf16[4,1,2,512,448]{3,4,2,1,0:T(8,128)(2,1)} %param.8), kind=kOutput, calls=%fused_computation.21 | convolution fusion | flops 16514176 | bytes 2821632 | tf_op jit(solution)/shard_map/...ik,...kj->...ij/dot_general | solution.py:52
  63.7 4.2 %all-to-all-start.2 = ((f32[8,1,1024]{2,1,0:T(1,128)}), f32[8,1,1024]{2,1,0:T(1,128)S(1)}, u32[]{:S(2)}, u32[]{:S(2)}) async-start(f32[8,1,1024]{2,1,0:T(1,128)} %broadcast_in_dim.20), calls=%async_computation.2 | async-start | bytes 65536 | tf_op jit(solution)/shard_map/all_to_all | solution.py:11
  68.3 1.4 %multiply_reduce_fusion.6 = (f32[128]{0:T(128)S(1)}, f32[1792,128]{0,1:T(8,128)S(1)}) fusion(bf16[1792,16]{0,1:T(8,128)(2,1)S(1)} %reshape.385, bf16[1,1,16,128]{3,0,2,1:T(2,128)(2,1)S(1)} %get-tuple-element.35, bf16[1,1,1792,128]{2,3,1,0:T(8,128)(2,1)} %copy.108), kind=kOutput, calls=%fused_computation.32 | convolution fusion | flops 8257408 | bytes 1438208 | tf_op jit(solution)/shard_map/...ik,...kj->...ij/dot_general | solution.py:52
  69.7 1.2 %multiply_reduce_fusion.4 = (f32[128]{0:T(128)S(1)}, f32[1792,128]{0,1:T(8,128)}) fusion(bf16[1792,16]{0,1:T(8,128)(2,1)S(1)} %reshape.395, bf16[1,1,16,128]{3,0,2,1:T(2,128)(2,1)S(1)} %get-tuple-element.33, bf16[1,1,1792,128]{2,3,1,0:T(8,128)(2,1)S(1)} %copy.110), kind=kOutput, calls=%fused_computation.30 | convolution fusion | flops 8257408 | bytes 1438208 | tf_op jit(solution)/shard_map/...ik,...kj->...ij/dot_general | solution.py:52
  71.0 1.6 %all-to-all-done.2 = f32[8,1,1024]{2,1,0:T(1,128)S(1)} async-done(((f32[8,1,1024]{2,1,0:T(1,128)}), f32[8,1,1024]{2,1,0:T(1,128)S(1)}, u32[]{:S(2)}, u32[]{:S(2)}) %all-to-all-start.2) | async-done | bytes 32800 | tf_op jit(solution)/shard_map/all_to_all | solution.py:11
  73.2 4.0 %all-to-all-start.4 = ((f32[8,1,1024]{2,1,0:T(1,128)}), f32[8,1,1024]{2,1,0:T(1,128)S(1)}, u32[]{:S(2)}, u32[]{:S(2)}) async-start(f32[8,1,1024]{2,1,0:T(1,128)} %broadcast_in_dim.22), calls=%async_computation.4 | async-start | bytes 65536 | tf_op jit(solution)/shard_map/all_to_all | solution.py:11
  77.2 4.7 %all-to-all-done.4 = f32[8,1,1024]{2,1,0:T(1,128)S(1)} async-done(((f32[8,1,1024]{2,1,0:T(1,128)}), f32[8,1,1024]{2,1,0:T(1,128)S(1)}, u32[]{:S(2)}, u32[]{:S(2)}) %all-to-all-start.4) | async-done | bytes 32800 | tf_op jit(solution)/shard_map/all_to_all | solution.py:11
  82.6 4.0 %all-to-all-start.3 = ((f32[8,1,1024]{2,1,0:T(1,128)}), f32[8,1,1024]{2,1,0:T(1,128)S(1)}, u32[]{:S(2)}, u32[]{:S(2)}) async-start(f32[8,1,1024]{2,1,0:T(1,128)} %broadcast_in_dim.21), calls=%async_computation.3 | async-start | bytes 65536 | tf_op jit(solution)/shard_map/all_to_all | solution.py:11
  86.6 4.7 %all-to-all-done.3 = f32[8,1,1024]{2,1,0:T(1,128)S(1)} async-done(((f32[8,1,1024]{2,1,0:T(1,128)}), f32[8,1,1024]{2,1,0:T(1,128)S(1)}, u32[]{:S(2)}, u32[]{:S(2)}) %all-to-all-start.3) | async-done | bytes 32800 | tf_op jit(solution)/shard_map/all_to_all | solution.py:11
  91.9 4.0 %all-to-all-start.5 = ((f32[8,1,1024]{2,1,0:T(1,128)}), f32[8,1,1024]{2,1,0:T(1,128)S(1)}, u32[]{:S(2)}, u32[]{:S(2)}) async-start(f32[8,1,1024]{2,1,0:T(1,128)} %broadcast_in_dim.23), calls=%async_computation.5 | async-start | bytes 65536 | tf_op jit(solution)/shard_map/all_to_all | solution.py:11
  96.1 4.5 %all-to-all-done.5 = f32[8,1,1024]{2,1,0:T(1,128)S(1)} async-done(((f32[8,1,1024]{2,1,0:T(1,128)}), f32[8,1,1024]{2,1,0:T(1,128)S(1)}, u32[]{:S(2)}, u32[]{:S(2)}) %all-to-all-start.5) | async-done | bytes 32800 | tf_op jit(solution)/shard_map/all_to_all | solution.py:11
  100.7 1.3 %fusion.10 = (bf16[1,1,1792,128]{2,3,1,0:T(8,128)(2,1)S(1)}, bf16[1,1,1792,128]{2,3,1,0:T(8,128)(2,1)S(1)}) fusion(f32[1792,128]{0,1:T(8,128)S(1)} %get-tuple-element.53, f32[128]{0:T(128)S(1)} %get-tuple-element.39, f32[1792,128]{0,1:T(8,128)} %get-tuple-element.49, f32[128]{0:T(128)S(1)} %get-tuple-element.38), kind=kLoop, calls=%fused_computation.36 | loop fusion | flops 917504 | bytes 2753536 | tf_op jit(solution)/shard_map/stack | solution.py:97
  102.5 2.3 %copy.98 = bf16[4,1,1792,128]{3,2,1,0:T(8,128)(2,1)} copy(bf16[4,1,1792,128]{2,3,1,0:T(8,128)(2,1)S(1)} %pad_maximum_fusion.1) | data formatting | bytes 3670016
  104.8 2.5 %fusion.6 = (bf16[1,1,2,512,448]{3,4,2,1,0:T(8,128)(2,1)S(1)}, bf16[1,1,2,512,448]{3,4,2,1,0:T(8,128)(2,1)S(1)}) fusion(f32[2,512,448]{1,2,0:T(8,128)} %get-tuple-element.55, f32[2,448]{1,0:T(2,128)S(1)} %get-tuple-element.31, f32[2,512,448]{1,2,0:T(8,128)} %get-tuple-element.51, f32[2,448]{1,0:T(2,128)S(1)} %get-tuple-element.30), kind=kLoop, calls=%fused_computation.24 | loop fusion | flops 1835008 | bytes 5512192 | tf_op jit(solution)/shard_map/stack | solution.py:97
  108.3 2.1 %pad_maximum_fusion = bf16[4,1,2,512,448]{3,4,2,1,0:T(8,128)(2,1)} fusion(bf16[1,1,2,512,448]{3,4,2,1,0:T(8,128)(2,1)S(1)} %get-tuple-element.59, bf16[1,1,2,512,448]{3,4,2,1,0:T(8,128)(2,1)S(1)} %get-tuple-element.58, bf16[1,1,2,512,448]{3,4,2,1,0:T(8,128)(2,1)S(1)} %get-tuple-element.57, bf16[1,1,2,512,448]{3,4,2,1,0:T(8,128)(2,1)S(1)} %get-tuple-element.56), kind=kLoop, calls=%fused_computation | loop fusion | flops 5505024 | bytes 7340032 | tf_op jit(solution)/shard_map/stack | solution.py:97
  (90 shorter events, 14.9 us)
Async XLA Ops:
  0.6 14.9 %copy-start = (bf16[4,1,56,16]{2,3,1,0:T(8,128)(2,1)S(1)}, bf16[4,1,56,16]{2,3,1,0:T(8,128)(2,1)}, u32[]{:S(2)}) copy-start(bf16[4,1,56,16]{2,3,1,0:T(8,128)(2,1)} %param.13) | copy-start | bytes 21508
  0.6 14.7 %copy-start.6 = (bf16[4,1,2,2,448]{4,3,2,1,0:T(2,128)(2,1)S(1)}, bf16[4,1,2,2,448]{4,3,2,1,0:T(2,128)(2,1)}, u32[]{:S(2)}) copy-start(bf16[4,1,2,2,448]{4,3,2,1,0:T(2,128)(2,1)} %param.10) | copy-start | bytes 43012
  3.5 33.0 %all-to-all-start = ((bf16[32,2,1024]{2,1,0:T(2,128)(2,1)}), bf16[32,2,1024]{2,1,0:T(2,128)(2,1)S(1)}, u32[]{:S(2)}, u32[]{:S(2)}) async-start(bf16[32,2,1024]{2,1,0:T(2,128)(2,1)} %reshape.406), calls=%async_computation | async-start | bytes 262144 | tf_op jit(solution)/shard_map/all_to_all | solution.py:11
  15.6 1.6 %copy-start.7 = (bf16[4,1,2,128]{3,2,1,0:T(2,128)(2,1)S(1)}, bf16[4,1,2,128]{3,2,1,0:T(2,128)(2,1)}, u32[]{:S(2)}) copy-start(bf16[4,1,2,128]{3,2,1,0:T(2,128)(2,1)} %param.14) | copy-start | bytes 6148
  36.6 24.1 %all-to-all-start.1 = ((bf16[32,2,1792]{2,1,0:T(2,128)(2,1)}), bf16[32,2,1792]{2,1,0:T(2,128)(2,1)S(1)}, u32[]{:S(2)}, u32[]{:S(2)}) async-start(bf16[32,2,1792]{2,1,0:T(2,128)(2,1)} %reshape.408), calls=%async_computation.1 | async-start | bytes 458752 | tf_op jit(solution)/shard_map/all_to_all | solution.py:11
  61.6 1.1 copy-start.4
  61.7 6.2 %copy-start.3 = (bf16[1,1,1792,128]{2,3,1,0:T(8,128)(2,1)S(1)}, bf16[1,1,1792,128]{2,3,1,0:T(8,128)(2,1)}, u32[]{:S(2)}) copy-start(bf16[1,1,1792,128]{2,3,1,0:T(8,128)(2,1)} %copy.109) | copy-start | bytes 1376260
  63.7 8.9 %all-to-all-start.2 = ((f32[8,1,1024]{2,1,0:T(1,128)}), f32[8,1,1024]{2,1,0:T(1,128)S(1)}, u32[]{:S(2)}, u32[]{:S(2)}) async-start(f32[8,1,1024]{2,1,0:T(1,128)} %broadcast_in_dim.20), calls=%async_computation.2 | async-start | bytes 65536 | tf_op jit(solution)/shard_map/all_to_all | solution.py:11
  68.3 32.3 %copy-start.8 = (f32[4,1,128]{2,1,0:T(1,128)S(1)}, f32[4,1,128]{2,1,0:T(1,128)}, u32[]{:S(2)}) copy-start(f32[4,1,128]{2,1,0:T(1,128)} %param.15) | copy-start | bytes 6148
  73.2 8.7 %all-to-all-start.4 = ((f32[8,1,1024]{2,1,0:T(1,128)}), f32[8,1,1024]{2,1,0:T(1,128)S(1)}, u32[]{:S(2)}, u32[]{:S(2)}) async-start(f32[8,1,1024]{2,1,0:T(1,128)} %broadcast_in_dim.22), calls=%async_computation.4 | async-start | bytes 65536 | tf_op jit(solution)/shard_map/all_to_all | solution.py:11
  82.6 8.7 %all-to-all-start.3 = ((f32[8,1,1024]{2,1,0:T(1,128)}), f32[8,1,1024]{2,1,0:T(1,128)S(1)}, u32[]{:S(2)}, u32[]{:S(2)}) async-start(f32[8,1,1024]{2,1,0:T(1,128)} %broadcast_in_dim.21), calls=%async_computation.3 | async-start | bytes 65536 | tf_op jit(solution)/shard_map/all_to_all | solution.py:11
  91.9 8.7 %all-to-all-start.5 = ((f32[8,1,1024]{2,1,0:T(1,128)}), f32[8,1,1024]{2,1,0:T(1,128)S(1)}, u32[]{:S(2)}, u32[]{:S(2)}) async-start(f32[8,1,1024]{2,1,0:T(1,128)} %broadcast_in_dim.23), calls=%async_computation.5 | async-start | bytes 65536 | tf_op jit(solution)/shard_map/all_to_all | solution.py:11
  102.5 2.3 %copy-start.5 = (f32[4,1,2,448]{3,2,1,0:T(2,128)S(1)}, f32[4,1,2,448]{3,2,1,0:T(2,128)}, u32[]{:S(2)}) copy-start(f32[4,1,2,448]{3,2,1,0:T(2,128)} %param.11) | copy-start | bytes 43012
  104.8 2.6 %copy-start.1 = (f32[2,512,448]{1,2,0:T(8,128)S(1)}, f32[2,512,448]{1,2,0:T(8,128)}, u32[]{:S(2)}) copy-start(f32[2,512,448]{1,2,0:T(8,128)} %get-tuple-element.47) | copy-start | bytes 5505028
  104.8 3.1 %copy-start.2 = (f32[2,512,448]{1,2,0:T(8,128)S(1)}, f32[2,512,448]{1,2,0:T(8,128)}, u32[]{:S(2)}) copy-start(f32[2,512,448]{1,2,0:T(8,128)} %get-tuple-element.43) | copy-start | bytes 5505028
where the time goes:
time: 111 us; the launch traced here: 110 us
  starting transfers between devices  37.4 us (34%)
  local copies, waits for them, and re-layouts  20.5 us (18%)
  waiting for transfers between devices  15.5 us (14%)
  matrix products  14.9 us (13%)
  blocking collectives  14.1 us (13%)
  other arithmetic  6.87 us (6%)
    all_to_all x6, starting transfers between devices, from_everyone(): lax.all_to_all(jnp.broadcast_to(value[None], (size, *value.shape)), axis,...  37.4 us
    all_to_all x6, waiting for transfers between devices, from_everyone(): lax.all_to_all(jnp.broadcast_to(value[None], (size, *value.shape)), axis,...  15.5 us
    dot_general x8, matrix products, combine_tile(): jnp.einsum('...ik,...kj->...ij', left, right, preferred_element_type=jnp....  14.9 us
    all_gather x1, blocking collectives, turned_gather(): lax.all_gather(both, axis, axis=0, tiled=True)  14.1 us
    unnamed x30, local copies, waits for them, and re-layouts  11.6 us
    another operation x6, other arithmetic, shards(): return (jnp.stack(inner_outputs), jnp.stack(outer_outputs))  6.63 us
    broadcast_in_dim x5, local copies, waits for them, and re-layouts, from_everyone(): jnp.broadcast_to(value[None], (size, *value.shape))  3.33 us
  transfers between devices with their start and end apart: 6, of which 4 were waited for; matrix products, arithmetic and copies ran while one was open for 23% of the time, Pallas kernels for 0%

commit v1 on v0

--- a/solution.py
+++ b/solution.py
@@ -40,7 +40,13 @@
 def turned_gather(arrays, axis, dims):
     turned = [jnp.moveaxis(a, dim, 0) for a, dim in zip(arrays, dims)]
     both = jnp.concatenate([t.reshape(len(t), -1) for t in turned], axis=1)
-    result, at, finished = (lax.all_gather(both, axis, axis=0, tiled=True), 0, [])
+    result, at, finished = (
+        jnp.concatenate(
+            lax.all_to_all(jnp.stack([both] * lax.axis_size(axis)), axis, 0, 0), axis=0
+        ),
+        0,
+        [],
+    )
     for t, dim in zip(turned, dims):
         section = result[:, at : at + t[0].size].reshape(-1, *t.shape[1:])
         finished.append(jnp.moveaxis(section, 0, dim))

time: 111 us -> 106 us (0.955)
  blocking collectives: 14.1 us -> 0 us
  waiting for transfers between devices: 15.5 us -> 20.1 us
  starting transfers between devices: 37.4 us -> 39.2 us
  local copies, waits for them, and re-layouts: 20.5 us -> 21.9 us
    all_gather x1 -> x0, blocking collectives: 14.1 us -> none  [turned_gather(): lax.all_gather(both, axis, axis=0, tiled=True)]
    all_to_all x0 -> x1, starting transfers between devices: none -> 6.47 us  [turned_gather(): lax.all_to_all(jnp.stack([both] * lax.axis_size(axis)), axis, 0, 0)]
    all_to_all x6, starting transfers between devices: 37.4 us -> 32.8 us  [from_everyone(): lax.all_to_all(jnp.broadcast_to(value[None], (size, *value.shape)), axis,...]
    all_to_all x6, waiting for transfers between devices: 15.5 us -> 19.3 us  [from_everyone(): lax.all_to_all(jnp.broadcast_to(value[None], (size, *value.shape)), axis,...]
    another operation x8 -> x9, local copies, waits for them, and re-layouts: 2.03 us -> 2.76 us
    unnamed x30 -> x25, local copies, waits for them, and re-layouts: 11.6 us -> 11.5 us
  transfers between devices with their start and end apart: 6 -> 7, of which waited for: 4 -> 6; matrix products, arithmetic and copies ran while one was open for 23% -> 26% of each run, Pallas kernels for 0% -> 0%
where the time goes in v1:
time: 106 us; the launch traced here: 105 us
  starting transfers between devices  39.2 us (37%)
  local copies, waits for them, and re-layouts  21.9 us (21%)
  waiting for transfers between devices  20.1 us (19%)
  matrix products  15 us (14%)
  other arithmetic  7.6 us (7%)
    all_to_all x6, starting transfers between devices, from_everyone(): lax.all_to_all(jnp.broadcast_to(value[None], (size, *value.shape)), axis,...  32.8 us
    all_to_all x6, waiting for transfers between devices, from_everyone(): lax.all_to_all(jnp.broadcast_to(value[None], (size, *value.shape)), axis,...  19.3 us
    dot_general x8, matrix products, combine_tile(): jnp.einsum('...ik,...kj->...ij', left, right, preferred_element_type=jnp....  15 us
    unnamed x25, local copies, waits for them, and re-layouts  11.5 us
    another operation x6, other arithmetic, shards(): return (jnp.stack(inner_outputs), jnp.stack(outer_outputs))  6.68 us
    all_to_all x1, starting transfers between devices, turned_gather(): lax.all_to_all(jnp.stack([both] * lax.axis_size(axis)), axis, 0, 0)  6.47 us
    broadcast_in_dim x5, local copies, waits for them, and re-layouts, from_everyone(): jnp.broadcast_to(value[None], (size, *value.shape))  3.32 us
  transfers between devices with their start and end apart: 7, of which 6 were waited for; matrix products, arithmetic and copies ran while one was open for 26% of the time, Pallas kernels for 0%

profile of v1, /device:TPU:1, one launch (start us, length us, event | category | flops | bytes accessed | tf_op | source)
XLA Modules:
  0.0 104.9 jit_solution(18319783553670352044)
XLA Ops:
  2.9 6.5 %all-to-all-start = ((bf16[8,2,4096]{2,1,0:T(2,128)(2,1)}), bf16[8,2,4096]{2,1,0:T(2,128)(2,1)S(1)}, u32[]{:S(2)}, u32[]{:S(2)}) async-start(bf16[8,2,4096]{2,1,0:T(2,128)(2,1)} %stack.41), calls=%async_computation | async-start | bytes 262144 | tf_op jit(solution)/shard_map/all_to_all | solution.py:45
  10.2 1.6 %fusion.20 = (bf16[1,1,1792,128]{3,2,1,0:T(8,128)(2,1)S(1)}, bf16[1,1,1792,128]{3,2,1,0:T(8,128)(2,1)S(1)}, bf16[1,1,1792,128]{3,2,1,0:T(8,128)(2,1)S(1)}, bf16[1,1,1792,128]{3,2,1,0:T(8,128)(2,1)S(1)}) fusion(bf16[4,1,1792,128]{3,2,1,0:T(8,128)(2,1)} %param.12), kind=kLoop, calls=%fused_computation.68 | loop fusion | bytes 3670016 | tf_op jit(solution)/shard_map/slice | solution.py:93
  12.0 1.8 %reshape.410 = bf16[32,2,1024]{2,1,0:T(2,128)(2,1)} reshape(bf16[32,4,1,2,16,16]{5,4,3,2,1,0:T(8,128)(2,1)S(1)} %broadcast_bitcast_fusion) | data formatting | bytes 262144
  14.7 10.5 %all-to-all-start.1 = ((bf16[32,2,1024]{2,1,0:T(2,128)(2,1)}), bf16[32,2,1024]{2,1,0:T(2,128)(2,1)S(1)}, u32[]{:S(2)}, u32[]{:S(2)}) async-start(bf16[32,2,1024]{2,1,0:T(2,128)(2,1)} %reshape.410), calls=%async_computation.1 | async-start | bytes 262144 | tf_op jit(solution)/shard_map/all_to_all | solution.py:11
  25.3 1.7 %reshape.412 = bf16[32,2,1792]{2,1,0:T(2,128)(2,1)} reshape(bf16[32,4,1,16,56]{4,3,2,1,0:T(8,128)(2,1)S(1)} %broadcast_bitcast_fusion.1) | data formatting | bytes 458752
  30.5 3.8 %all-to-all-done.1 = bf16[32,2,1024]{2,1,0:T(2,128)(2,1)S(1)} async-done(((bf16[32,2,1024]{2,1,0:T(2,128)(2,1)}), bf16[32,2,1024]{2,1,0:T(2,128)(2,1)S(1)}, u32[]{:S(2)}, u32[]{:S(2)}) %all-to-all-start.1) | async-done | bytes 131104 | tf_op jit(solution)/shard_map/all_to_all | solution.py:11
  34.3 5.4 %all-to-all-start.2 = ((bf16[32,2,1792]{2,1,0:T(2,128)(2,1)}), bf16[32,2,1792]{2,1,0:T(2,128)(2,1)S(1)}, u32[]{:S(2)}, u32[]{:S(2)}) async-start(bf16[32,2,1792]{2,1,0:T(2,128)(2,1)} %reshape.412), calls=%async_computation.2 | async-start | bytes 458752 | tf_op jit(solution)/shard_map/all_to_all | solution.py:11
  42.5 2.9 %multiply_reduce_fusion.2 = (f32[2,448]{1,0:T(2,128)S(1)}, f32[2,512,448]{1,2,0:T(8,128)}) fusion(bf16[2,512,16]{1,2,0:T(8,128)(2,1)S(1)} %reshape.388, bf16[4,1,2,16,448]{4,3,2,1,0:T(8,128)(2,1)S(1)} %bitcast.185, bf16[4,1,2,512,448]{3,4,2,1,0:T(8,128)(2,1)} %param.8), kind=kOutput, calls=%fused_computation.19 | convolution fusion | flops 16514176 | bytes 2821632 | tf_op jit(solution)/shard_map/...ik,...kj->...ij/dot_general | solution.py:58
  45.5 2.9 %multiply_reduce_fusion.1 = (f32[2,448]{1,0:T(2,128)S(1)}, f32[2,512,448]{1,2,0:T(8,128)}) fusion(bf16[2,512,16]{1,2,0:T(8,128)(2,1)S(1)} %reshape.393, bf16[4,1,2,16,448]{4,3,2,1,0:T(8,128)(2,1)S(1)} %bitcast.186, bf16[4,1,2,512,448]{3,4,2,1,0:T(8,128)(2,1)} %param.8), kind=kOutput, calls=%fused_computation.17 | convolution fusion | flops 16514176 | bytes 2821632 | tf_op jit(solution)/shard_map/...ik,...kj->...ij/dot_general | solution.py:58
  48.4 2.9 %multiply_reduce_fusion = (f32[2,448]{1,0:T(2,128)S(1)}, f32[2,512,448]{1,2,0:T(8,128)}) fusion(bf16[2,512,16]{1,2,0:T(8,128)(2,1)S(1)} %reshape.398, bf16[4,1,2,16,448]{4,3,2,1,0:T(8,128)(2,1)S(1)} %bitcast.187, bf16[4,1,2,512,448]{3,4,2,1,0:T(8,128)(2,1)} %param.8), kind=kOutput, calls=%fused_computation.15 | convolution fusion | flops 16514176 | bytes 2821632 | tf_op jit(solution)/shard_map/...ik,...kj->...ij/dot_general | solution.py:58
  51.4 2.9 %multiply_reduce_fusion.3 = (f32[2,448]{1,0:T(2,128)S(1)}, f32[2,512,448]{1,2,0:T(8,128)}) fusion(bf16[2,512,16]{1,2,0:T(8,128)(2,1)S(1)} %reshape.382, bf16[4,1,2,16,448]{4,3,2,1,0:T(8,128)(2,1)S(1)} %bitcast.188, bf16[4,1,2,512,448]{3,4,2,1,0:T(8,128)(2,1)} %param.8), kind=kOutput, calls=%fused_computation.21 | convolution fusion | flops 16514176 | bytes 2821632 | tf_op jit(solution)/shard_map/...ik,...kj->...ij/dot_general | solution.py:58
  57.4 4.9 %all-to-all-start.3 = ((f32[8,1,1024]{2,1,0:T(1,128)}), f32[8,1,1024]{2,1,0:T(1,128)S(1)}, u32[]{:S(2)}, u32[]{:S(2)}) async-start(f32[8,1,1024]{2,1,0:T(1,128)} %broadcast_in_dim.20), calls=%async_computation.3 | async-start | bytes 65536 | tf_op jit(solution)/shard_map/all_to_all | solution.py:11
  62.7 1.4 %multiply_reduce_fusion.6 = (f32[128]{0:T(128)S(1)}, f32[1792,128]{0,1:T(8,128)S(1)}) fusion(bf16[1792,16]{0,1:T(8,128)(2,1)S(1)} %reshape.391, bf16[1,1,16,128]{3,0,2,1:T(2,128)(2,1)S(1)} %get-tuple-element.35, bf16[1,1,1792,128]{2,3,1,0:T(8,128)(2,1)} %copy.108), kind=kOutput, calls=%fused_computation.32 | convolution fusion | flops 8257408 | bytes 1438208 | tf_op jit(solution)/shard_map/...ik,...kj->...ij/dot_general | solution.py:58
  65.4 1.6 %all-to-all-done.3 = f32[8,1,1024]{2,1,0:T(1,128)S(1)} async-done(((f32[8,1,1024]{2,1,0:T(1,128)}), f32[8,1,1024]{2,1,0:T(1,128)S(1)}, u32[]{:S(2)}, u32[]{:S(2)}) %all-to-all-start.3) | async-done | bytes 32800 | tf_op jit(solution)/shard_map/all_to_all | solution.py:11
  67.7 4.0 %all-to-all-start.5 = ((f32[8,1,1024]{2,1,0:T(1,128)}), f32[8,1,1024]{2,1,0:T(1,128)S(1)}, u32[]{:S(2)}, u32[]{:S(2)}) async-start(f32[8,1,1024]{2,1,0:T(1,128)} %broadcast_in_dim.22), calls=%async_computation.5 | async-start | bytes 65536 | tf_op jit(solution)/shard_map/all_to_all | solution.py:11
  71.7 4.7 %all-to-all-done.5 = f32[8,1,1024]{2,1,0:T(1,128)S(1)} async-done(((f32[8,1,1024]{2,1,0:T(1,128)}), f32[8,1,1024]{2,1,0:T(1,128)S(1)}, u32[]{:S(2)}, u32[]{:S(2)}) %all-to-all-start.5) | async-done | bytes 32800 | tf_op jit(solution)/shard_map/all_to_all | solution.py:11
  77.0 4.0 %all-to-all-start.4 = ((f32[8,1,1024]{2,1,0:T(1,128)}), f32[8,1,1024]{2,1,0:T(1,128)S(1)}, u32[]{:S(2)}, u32[]{:S(2)}) async-start(f32[8,1,1024]{2,1,0:T(1,128)} %broadcast_in_dim.21), calls=%async_computation.4 | async-start | bytes 65536 | tf_op jit(solution)/shard_map/all_to_all | solution.py:11
  81.0 4.7 %all-to-all-done.4 = f32[8,1,1024]{2,1,0:T(1,128)S(1)} async-done(((f32[8,1,1024]{2,1,0:T(1,128)}), f32[8,1,1024]{2,1,0:T(1,128)S(1)}, u32[]{:S(2)}, u32[]{:S(2)}) %all-to-all-start.4) | async-done | bytes 32800 | tf_op jit(solution)/shard_map/all_to_all | solution.py:11
  86.3 4.0 %all-to-all-start.6 = ((f32[8,1,1024]{2,1,0:T(1,128)}), f32[8,1,1024]{2,1,0:T(1,128)S(1)}, u32[]{:S(2)}, u32[]{:S(2)}) async-start(f32[8,1,1024]{2,1,0:T(1,128)} %broadcast_in_dim.23), calls=%async_computation.6 | async-start | bytes 65536 | tf_op jit(solution)/shard_map/all_to_all | solution.py:11
  90.5 4.5 %all-to-all-done.6 = f32[8,1,1024]{2,1,0:T(1,128)S(1)} async-done(((f32[8,1,1024]{2,1,0:T(1,128)}), f32[8,1,1024]{2,1,0:T(1,128)S(1)}, u32[]{:S(2)}, u32[]{:S(2)}) %all-to-all-start.6) | async-done | bytes 32800 | tf_op jit(solution)/shard_map/all_to_all | solution.py:11
  95.2 1.3 %fusion.10 = (bf16[1,1,1792,128]{2,3,1,0:T(8,128)(2,1)S(1)}, bf16[1,1,1792,128]{2,3,1,0:T(8,128)(2,1)S(1)}) fusion(f32[1792,128]{0,1:T(8,128)S(1)} %get-tuple-element.53, f32[128]{0:T(128)S(1)} %get-tuple-element.39, f32[1792,128]{0,1:T(8,128)} %get-tuple-element.49, f32[128]{0:T(128)S(1)} %get-tuple-element.38), kind=kLoop, calls=%fused_computation.36 | loop fusion | flops 917504 | bytes 2753536 | tf_op jit(solution)/shard_map/stack | solution.py:103
  96.9 2.3 %copy.98 = bf16[4,1,1792,128]{3,2,1,0:T(8,128)(2,1)} copy(bf16[4,1,1792,128]{2,3,1,0:T(8,128)(2,1)S(1)} %pad_maximum_fusion.1) | data formatting | bytes 3670016
  99.3 2.5 %fusion.6 = (bf16[1,1,2,512,448]{3,4,2,1,0:T(8,128)(2,1)S(1)}, bf16[1,1,2,512,448]{3,4,2,1,0:T(8,128)(2,1)S(1)}) fusion(f32[2,512,448]{1,2,0:T(8,128)} %get-tuple-element.55, f32[2,448]{1,0:T(2,128)S(1)} %get-tuple-element.31, f32[2,512,448]{1,2,0:T(8,128)} %get-tuple-element.51, f32[2,448]{1,0:T(2,128)S(1)} %get-tuple-element.30), kind=kLoop, calls=%fused_computation.24 | loop fusion | flops 1835008 | bytes 5512192 | tf_op jit(solution)/shard_map/stack | solution.py:103
  102.8 2.1 %pad_maximum_fusion = bf16[4,1,2,512,448]{3,4,2,1,0:T(8,128)(2,1)} fusion(bf16[1,1,2,512,448]{3,4,2,1,0:T(8,128)(2,1)S(1)} %get-tuple-element.59, bf16[1,1,2,512,448]{3,4,2,1,0:T(8,128)(2,1)S(1)} %get-tuple-element.58, bf16[1,1,2,512,448]{3,4,2,1,0:T(8,128)(2,1)S(1)} %get-tuple-element.57, bf16[1,1,2,512,448]{3,4,2,1,0:T(8,128)(2,1)S(1)} %get-tuple-element.56), kind=kLoop, calls=%fused_computation | loop fusion | flops 5505024 | bytes 7340032 | tf_op jit(solution)/shard_map/stack | solution.py:103
  (88 shorter events, 19.1 us)
Async XLA Ops:
  0.6 24.5 %copy-start = (bf16[4,1,56,16]{2,3,1,0:T(8,128)(2,1)S(1)}, bf16[4,1,56,16]{2,3,1,0:T(8,128)(2,1)}, u32[]{:S(2)}) copy-start(bf16[4,1,56,16]{2,3,1,0:T(8,128)(2,1)} %param.13) | copy-start | bytes 21508
  2.9 11.7 %all-to-all-start = ((bf16[8,2,4096]{2,1,0:T(2,128)(2,1)}), bf16[8,2,4096]{2,1,0:T(2,128)(2,1)S(1)}, u32[]{:S(2)}, u32[]{:S(2)}) async-start(bf16[8,2,4096]{2,1,0:T(2,128)(2,1)} %stack.41), calls=%async_computation | async-start | bytes 262144 | tf_op jit(solution)/shard_map/all_to_all | solution.py:45
  14.7 19.7 %all-to-all-start.1 = ((bf16[32,2,1024]{2,1,0:T(2,128)(2,1)}), bf16[32,2,1024]{2,1,0:T(2,128)(2,1)S(1)}, u32[]{:S(2)}, u32[]{:S(2)}) async-start(bf16[32,2,1024]{2,1,0:T(2,128)(2,1)} %reshape.410), calls=%async_computation.1 | async-start | bytes 262144 | tf_op jit(solution)/shard_map/all_to_all | solution.py:11
  34.3 20.1 %all-to-all-start.2 = ((bf16[32,2,1792]{2,1,0:T(2,128)(2,1)}), bf16[32,2,1792]{2,1,0:T(2,128)(2,1)S(1)}, u32[]{:S(2)}, u32[]{:S(2)}) async-start(bf16[32,2,1792]{2,1,0:T(2,128)(2,1)} %reshape.412), calls=%async_computation.2 | async-start | bytes 458752 | tf_op jit(solution)/shard_map/all_to_all | solution.py:11
  55.3 1.1 %copy-start.4 = (bf16[1,1,1792,128]{2,3,1,0:T(8,128)(2,1)S(1)}, bf16[1,1,1792,128]{2,3,1,0:T(8,128)(2,1)}, u32[]{:S(2)}) copy-start(bf16[1,1,1792,128]{2,3,1,0:T(8,128)(2,1)} %copy.107) | copy-start | bytes 1376260
  55.4 7.0 %copy-start.3 = (bf16[1,1,1792,128]{2,3,1,0:T(8,128)(2,1)S(1)}, bf16[1,1,1792,128]{2,3,1,0:T(8,128)(2,1)}, u32[]{:S(2)}) copy-start(bf16[1,1,1792,128]{2,3,1,0:T(8,128)(2,1)} %copy.109) | copy-start | bytes 1376260
  57.4 9.7 %all-to-all-start.3 = ((f32[8,1,1024]{2,1,0:T(1,128)}), f32[8,1,1024]{2,1,0:T(1,128)S(1)}, u32[]{:S(2)}, u32[]{:S(2)}) async-start(f32[8,1,1024]{2,1,0:T(1,128)} %broadcast_in_dim.20), calls=%async_computation.3 | async-start | bytes 65536 | tf_op jit(solution)/shard_map/all_to_all | solution.py:11
  62.7 32.3 %copy-start.6 = (f32[4,1,128]{2,1,0:T(1,128)S(1)}, f32[4,1,128]{2,1,0:T(1,128)}, u32[]{:S(2)}) copy-start(f32[4,1,128]{2,1,0:T(1,128)} %param.15) | copy-start | bytes 6148
  67.7 8.7 %all-to-all-start.5 = ((f32[8,1,1024]{2,1,0:T(1,128)}), f32[8,1,1024]{2,1,0:T(1,128)S(1)}, u32[]{:S(2)}, u32[]{:S(2)}) async-start(f32[8,1,1024]{2,1,0:T(1,128)} %broadcast_in_dim.22), calls=%async_computation.5 | async-start | bytes 65536 | tf_op jit(solution)/shard_map/all_to_all | solution.py:11
  77.0 8.7 %all-to-all-start.4 = ((f32[8,1,1024]{2,1,0:T(1,128)}), f32[8,1,1024]{2,1,0:T(1,128)S(1)}, u32[]{:S(2)}, u32[]{:S(2)}) async-start(f32[8,1,1024]{2,1,0:T(1,128)} %broadcast_in_dim.21), calls=%async_computation.4 | async-start | bytes 65536 | tf_op jit(solution)/shard_map/all_to_all | solution.py:11
  86.3 8.7 %all-to-all-start.6 = ((f32[8,1,1024]{2,1,0:T(1,128)}), f32[8,1,1024]{2,1,0:T(1,128)S(1)}, u32[]{:S(2)}, u32[]{:S(2)}) async-start(f32[8,1,1024]{2,1,0:T(1,128)} %broadcast_in_dim.23), calls=%async_computation.6 | async-start | bytes 65536 | tf_op jit(solution)/shard_map/all_to_all | solution.py:11
  96.9 2.3 %copy-start.5 = (f32[4,1,2,448]{3,2,1,0:T(2,128)S(1)}, f32[4,1,2,448]{3,2,1,0:T(2,128)}, u32[]{:S(2)}) copy-start(f32[4,1,2,448]{3,2,1,0:T(2,128)} %param.11) | copy-start | bytes 43012
  99.3 2.6 %copy-start.1 = (f32[2,512,448]{1,2,0:T(8,128)S(1)}, f32[2,512,448]{1,2,0:T(8,128)}, u32[]{:S(2)}) copy-start(f32[2,512,448]{1,2,0:T(8,128)} %get-tuple-element.47) | copy-start | bytes 5505028
  99.3 3.1 %copy-start.2 = (f32[2,512,448]{1,2,0:T(8,128)S(1)}, f32[2,512,448]{1,2,0:T(8,128)}, u32[]{:S(2)}) copy-start(f32[2,512,448]{1,2,0:T(8,128)} %get-tuple-element.43) | copy-start | bytes 5505028
